TPU v7x, 32 devices: a whole 2x2x4 slice. The times are simulated.
32 devices in a mesh: grp: 8 (over y, x, core), sp: 4 (over z).
Axes of the slice: x: 2, y: 2, z: 4, core: 2. Of those that a mesh axis runs over, the one named last changes fastest.
Arguments:
- latents: bfloat16 [8, 512, 3072], P('grp', 'sp'), may hold values from -6 to 6
- timestep: int32 [8], P('grp'), may hold values from 0 to 999
- w_mod: bfloat16 [256, 9216], replicated, may hold values from -0.375 to 0.375
- w_qkv: bfloat16 [4, 3072, 384], P('sp', 'grp'), may hold values from -2 to 2
- w_out: bfloat16 [4, 128, 3072], P('sp', 'grp'), may hold values from -0.5 to 0.5
Outputs:
- update: bfloat16 [8, 512, 3072], P('grp', 'sp')
All inputs are finite; a program needn't handle non-finite values.
Results may differ from a plain program's by a relative error of at most 0.012.
Values may be sent and summed in bfloat16 or wider, within the bound.
No kernel may reach another device: no remote copies, remote signals or barrier semaphores. Data moves between devices by JAX's collectives and lax.ppermute only.
A program may use at most 128 MiB of HBM per device.

v0:
```python
import functools
import math

import jax
import jax.numpy as jnp
from jax import lax
from jax.experimental import pallas as pl
from jax.experimental.pallas import tpu as pltpu
from jax.sharding import PartitionSpec as P


AXES = ("grp", "sp")


def modulation(timestep, w_mod):
    half_freq = w_mod.shape[0] // 2
    freqs = jnp.exp(-math.log(10000.0) * jnp.arange(half_freq, dtype=jnp.float32) / half_freq)
    angles = timestep.astype(jnp.float32)[:, None] * freqs[None, :]
    embed = jnp.concatenate([jnp.cos(angles), jnp.sin(angles)], axis=1).astype(jnp.bfloat16)
    return jnp.dot(embed, w_mod, preferred_element_type=jnp.float32)


def normalize(latents, shift, scale):
    values = latents.astype(jnp.float32)
    center = jnp.mean(values, axis=-1, keepdims=True)
    spread = jnp.mean((values - center) ** 2, axis=-1, keepdims=True)
    normed = (values - center) * lax.rsqrt(spread + 1e-06)
    return (normed * (1.0 + scale) + shift).astype(jnp.bfloat16)


def project_kernel(chunks, owner_ref, reorder_ref, *refs):
    xs, pieces, (query_ref, kv_ref) = refs[:chunks], refs[chunks:-2], refs[-2:]
    head_size = query_ref.shape[1]
    tokens = xs[0].shape[0]
    for chunk, x_ref in enumerate(xs):
        total = jnp.zeros((tokens, 3 * head_size), jnp.float32)
        for index, piece in enumerate(pieces):
            rows = piece.shape[0]
            start = pl.multiple_of(owner_ref[index] * rows, 128)
            total += jnp.dot(x_ref[:, pl.ds(start, rows)], piece[...], preferred_element_type=jnp.float32)
        qkv = total.astype(jnp.bfloat16)
        values = jnp.dot(qkv[:, 2 * head_size :], reorder_ref[...], preferred_element_type=jnp.float32)
        place = pl.ds(chunk * tokens, tokens)
        query_ref[place, :] = qkv[:, :head_size]
        kv_ref[place, :head_size] = qkv[:, head_size : 2 * head_size]
        kv_ref[place, head_size:] = values.astype(jnp.bfloat16)


def project(xs, pieces, owners, reorder):
    rows, columns = pieces[0].shape
    head_size = columns // 3
    if rows % 128:
        x = jnp.concatenate(xs, axis=0)
        total = jnp.zeros((x.shape[0], columns), jnp.float32)
        for index, piece in enumerate(pieces):
            part = lax.dynamic_slice_in_dim(x, owners[index] * rows, rows, axis=1)
            total += jnp.dot(part, piece, preferred_element_type=jnp.float32)
        qkv = total.astype(jnp.bfloat16)
        values = jnp.dot(qkv[:, 2 * head_size :], reorder, preferred_element_type=jnp.float32)
        kv = jnp.concatenate([qkv[:, head_size : 2 * head_size], values.astype(jnp.bfloat16)], axis=1)
        return qkv[:, :head_size], kv
    vmem = pl.BlockSpec(memory_space=pltpu.VMEM)
    tokens = sum(x.shape[0] for x in xs)
    return pl.pallas_call(
        functools.partial(project_kernel, len(xs)),
        out_shape=(
            jax.ShapeDtypeStruct((tokens, head_size), jnp.bfloat16),
            jax.ShapeDtypeStruct((tokens, 2 * head_size), jnp.bfloat16),
        ),
        in_specs=[pl.BlockSpec(memory_space=pltpu.SMEM)] + [vmem] * (1 + len(xs) + len(pieces)),
        out_specs=(vmem, vmem),
        compiler_params=pltpu.CompilerParams(vmem_limit_bytes=16 * 2**20),
        cost_estimate=pl.CostEstimate(
            flops=2 * tokens * xs[0].shape[1] * columns,
            bytes_accessed=2 * (tokens + columns) * xs[0].shape[1],
            transcendentals=0,
        ),
    )(owners, reorder, *xs, *pieces)


def after(value, *ready):
    return lax.optimization_barrier((value,) + ready)[0]


def attend(query, keys, values):
    head_size = query.shape[1]
    scores = lax.dot_general(query, keys, (((1,), (1,)), ((), ())), preferred_element_type=jnp.float32)
    scores = scores / math.sqrt(head_size)
    largest = jnp.max(scores, axis=1, keepdims=True)
    weights = jnp.exp(scores - largest)
    probs = (weights / jnp.sum(weights, axis=1, keepdims=True)).astype(jnp.bfloat16)
    return jnp.dot(probs, values, preferred_element_type=jnp.float32).astype(jnp.bfloat16)


def on_device(groups, spread, latents, timestep, w_mod, w_qkv, w_out):
    _, tok_local, width = latents.shape
    head_size = w_qkv.shape[2] // 3
    half = spread // 2
    chips = groups // 2
    grp = lax.axis_index("grp")

    def move(value, grp_to, sp_to):
        pairs = []
        for g in range(groups):
            for s in range(spread):
                pairs.append((g * spread + s, grp_to(g) * spread + sp_to(s)))
        return lax.ppermute(value, AXES, pairs)

    def sp_shift(across, along):
        def to(s):
            return (s // half + across) % 2 * half + (s % half + along) % half

        return to

    def chip_step(step):
        if chips & (chips - 1) == 0:
            return lambda g: ((g // 2) ^ step) * 2 + g % 2
        return lambda g: (g // 2 - step) % chips * 2 + g % 2

    def chip_owner(step):
        if chips & (chips - 1) == 0:
            return (grp // 2) ^ step
        return (grp // 2 + step) % chips

    same = lambda index: index
    partner = lambda g: g ^ 1

    def over_chips(value):
        return [value] + [move(value, chip_step(step), same) for step in range(1, chips)]

    def over_cores(pieces):
        return pieces + [move(piece, partner, same) for piece in pieces]

    owners = jnp.stack(
        [chip_owner(step) * 2 + (grp % 2 + flip) % 2 for flip in range(2) for step in range(chips)]
    ).astype(jnp.int32)

    rows_each = head_size // groups
    column = jnp.arange(head_size, dtype=jnp.int32)
    source = jnp.repeat(owners, rows_each) * rows_each + column % rows_each
    reorder = (column[:, None] == source[None, :]).astype(jnp.bfloat16)

    raw = [latents[0]] + [move(latents[0], same, sp_shift(0, -step)) for step in range(1, half)]
    other_shard = move(w_qkv[0], same, sp_shift(1, 0))
    own_in = over_chips(w_qkv[0])

    mod = modulation(timestep, w_mod)
    shift, scale, gate = mod[:, :width], mod[:, width : 2 * width], mod[:, 2 * width :]
    mine_normed = normalize(raw[0], shift, scale)

    other_in = over_chips(after(other_shard, mine_normed))
    own_pieces = over_cores(own_in)
    out_shards = []
    out_shard = after(w_out[0], mine_normed)
    for step in range(half):
        for across in range(2):
            shard = out_shard
            if step or across:
                shard = move(shard, same, sp_shift(across, step))
            out_shards.append(shard)

    xs = [mine_normed] + [normalize(rows, shift, scale) for rows in after(raw, mine_normed)[1:]]

    queries, local_kv, remote_kv = [], [], []
    for pieces in (own_pieces, None):
        if pieces is None:
            other_in = after(other_in, local_kv[0])
            out_mine = over_chips(after(jnp.stack(out_shards), local_kv[0]))
            pieces = over_cores(other_in)
        query, kv = project(xs, pieces, owners, reorder)
        queries.append(query)
        local_kv.append(kv)
        remote_kv.append(move(kv, same, sp_shift(1, 0)))
    out_pieces = over_cores(after(out_mine, local_kv[1]))

    heads = [None, None]
    for index in (1, 0):
        kv = jnp.concatenate([local_kv[index], remote_kv[1 - index]], axis=0)
        heads[index] = attend(queries[index], kv[:, :head_size], kv[:, head_size:])
    both = jnp.concatenate(heads, axis=1)

    mine = []
    for step in range(half):
        part = both[step * tok_local : (step + 1) * tok_local]
        if step:
            part = move(part, same, sp_shift(0, step))
        mine.append(part)
    attended = jnp.concatenate(mine, axis=1)
    rows = jnp.concatenate(out_pieces, axis=1).reshape(attended.shape[1], width)
    total = jnp.dot(attended, rows, preferred_element_type=jnp.float32)
    return (gate * total).astype(jnp.bfloat16)[None]


def solution(mesh):
    placed = (P("grp", "sp", None), P("grp"), P(), P("sp", "grp", None), P("sp", "grp", None))

    def body(*args):
        return on_device(mesh.shape["grp"], mesh.shape["sp"], *args)

    return jax.shard_map(
        body, mesh=mesh, in_specs=placed, out_specs=P("grp", "sp", None), check_vma=False
    )
```

profile of v0, /device:TPU:0, one launch (start us, length us, event | category | flops | bytes accessed | tf_op | source)
XLA Modules:
  0.0 85.3 jit_solution(5923603913345964359)
XLA Ops:
  0.0 3.0 %collective-permute-start.1 = (bf16[384,384]{1,0:T(8,128)(2,1)}, bf16[384,384]{1,0:T(8,128)(2,1)S(1)}, u32[]{:S(2)}, u32[]{:S(2)}) collective-permute-start(bf16[384,384]{1,0:T(8,128)(2,1)} %bitcast.31), channel_id=1, source_target_pairs={{0,8},{1,9},{2,10},{3,11},{4,12},{5,13},{6,14},{7,15},{8,0},{9,1},... | collective-permute-start | bytes 884744 | tf_op jit(solution)/shard_map/ppermute | solution.py:107
  3.0 1.5 %collective-permute-start.2 = (bf16[384,384]{1,0:T(8,128)(2,1)}, bf16[384,384]{1,0:T(8,128)(2,1)S(1)}, u32[]{:S(2)}, u32[]{:S(2)}) collective-permute-start(bf16[384,384]{1,0:T(8,128)(2,1)} %bitcast.32), channel_id=1, source_target_pairs={{0,16},{1,17},{2,18},{3,19},{4,20},{5,21},{6,22},{7,23},{8,24},{9,... | collective-permute-start | bytes 884744 | tf_op jit(solution)/shard_map/ppermute | solution.py:107
  4.5 3.1 %collective-permute-start.8 = (bf16[384,384]{1,0:T(8,128)(2,1)}, bf16[384,384]{1,0:T(8,128)(2,1)S(1)}, u32[]{:S(2)}, u32[]{:S(2)}) collective-permute-start(bf16[384,384]{1,0:T(8,128)(2,1)} %bitcast.34), channel_id=1, source_target_pairs={{0,2},{1,3},{2,0},{3,1},{4,6},{5,7},{6,4},{7,5},{8,10},{9,11},{10,... | collective-permute-start | bytes 884744 | tf_op jit(solution)/shard_map/ppermute | solution.py:107
  7.6 1.6 %collective-permute-start = (bf16[128,3072]{1,0:T(8,128)(2,1)}, bf16[128,3072]{1,0:T(8,128)(2,1)}, u32[]{:S(2)}, u32[]{:S(2)}) collective-permute-start(bf16[128,3072]{1,0:T(8,128)(2,1)} %bitcast.37), channel_id=1, source_target_pairs={{0,1},{1,0},{2,3},{3,2},{4,5},{5,4},{6,7},{7,6},{8,9},{9,8},{10,11... | collective-permute-start | bytes 2359304 | tf_op jit(solution)/shard_map/ppermute | solution.py:107
  9.1 1.4 %convert_reduce_fusion.1 = f32[128]{0:T(128)S(1)} fusion(bf16[1,128,3072]{2,1,0:T(8,128)(2,1)} %param.5), kind=kLoop, calls=%fused_computation.6 | loop fusion | flops 786304 | bytes 786944 | tf_op jit(solution)/shard_map/reduce_sum | solution.py:25
  11.2 3.1 %fusion.30 = f32[1,9216]{1,0:T(1,128)S(1)} fusion(bf16[256,1]{0,1:T(2,128)(2,1)S(1)} %reshape.69, bf16[256,9216]{1,0:T(8,128)(2,1)} %param.7), kind=kOutput, calls=%fused_computation.71 | convolution fusion | flops 4718592 | bytes 4755968 | tf_op jit(solution)/shard_map/dot_general | solution.py:20
  14.4 0.4 fusion.10
  14.8 0.4 fusion.13.refs_0_
  15.2 0.1 stack.50.owner_ref
  15.5 4.9 %collective-permute-done.8.refs_2_ = bf16[384,384]{1,0:T(8,128)(2,1)S(1)} collective-permute-done((bf16[384,384]{1,0:T(8,128)(2,1)}, bf16[384,384]{1,0:T(8,128)(2,1)S(1)}, u32[]{:S(2)}, u32[]{:S(2)}) %collective-permute-start.8) | collective-permute-done | bytes 294944 | tf_op jit(solution)/shard_map/ppermute | solution.py:107
  20.4 1.6 %collective-permute-start.10 = (bf16[384,384]{1,0:T(8,128)(2,1)S(1)}, bf16[384,384]{1,0:T(8,128)(2,1)S(1)}, u32[]{:S(2)}, u32[]{:S(2)}) collective-permute-start(bf16[384,384]{1,0:T(8,128)(2,1)S(1)} %collective-permute-done.8.refs_2_), channel_id=1, source_target_pairs={{0,16},{1,17},{2,18},{3,19},{4,20},{5,21},{6,22},{7,23},{8,24},{9,... | collective-permute-start | bytes 884744 | tf_op jit(solution)/shard_map/ppermute | solution.py:107
  22.0 0.2 collective-permute-start.5
  22.2 0.4 collective-permute-start.6
  22.5 8.7 %collective-permute-done = bf16[128,3072]{1,0:T(8,128)(2,1)} collective-permute-done((bf16[128,3072]{1,0:T(8,128)(2,1)}, bf16[128,3072]{1,0:T(8,128)(2,1)}, u32[]{:S(2)}, u32[]{:S(2)}) %collective-permute-start) | collective-permute-done | bytes 786464 | tf_op jit(solution)/shard_map/ppermute | solution.py:107
  31.2 1.3 %convert_reduce_fusion = f32[128]{0:T(128)S(1)} fusion(bf16[128,3072]{1,0:T(8,128)(2,1)} %collective-permute-done), kind=kLoop, calls=%fused_computation.4 | loop fusion | flops 786304 | bytes 786944 | tf_op jit(solution)/shard_map/reduce_sum | solution.py:25
  32.5 1.5 %fusion.6 = f32[128]{0:T(128)S(1)} fusion(bf16[128,3072]{1,0:T(8,128)(2,1)} %collective-permute-done, f32[128]{0:T(128)S(1)} %broadcast_multiply_fusion), kind=kLoop, calls=%fused_computation.11 | loop fusion | flops 1572736 | bytes 787456 | tf_op jit(solution)/shard_map/reduce_sum | solution.py:26
  34.1 1.4 %collective-permute-start.19 = (bf16[16,3072]{1,0:T(8,128)(2,1)S(1)}, bf16[16,3072]{1,0:T(8,128)(2,1)S(1)}, u32[]{:S(2)}, u32[]{:S(2)}) collective-permute-start(bf16[16,3072]{1,0:T(8,128)(2,1)S(1)} %bitcast.43), channel_id=1, source_target_pairs={{0,2},{1,3},{2,0},{3,1},{4,6},{5,7},{6,4},{7,5},{8,10},{9,11},{10,... | collective-permute-start | bytes 294920 | tf_op jit(solution)/shard_map/ppermute | solution.py:107
  35.5 1.7 %collective-permute-start.20 = (bf16[16,3072]{1,0:T(8,128)(2,1)S(1)}, bf16[16,3072]{1,0:T(8,128)(2,1)S(1)}, u32[]{:S(2)}, u32[]{:S(2)}) collective-permute-start(bf16[16,3072]{1,0:T(8,128)(2,1)S(1)} %bitcast.44), channel_id=1, source_target_pairs={{0,1},{1,0},{2,3},{3,2},{4,5},{5,4},{6,7},{7,6},{8,9},{9,8},{10,11... | collective-permute-start | bytes 294920 | tf_op jit(solution)/shard_map/ppermute | solution.py:107
  37.2 1.3 %collective-permute-start.21 = (bf16[16,3072]{1,0:T(8,128)(2,1)S(1)}, bf16[16,3072]{1,0:T(8,128)(2,1)S(1)}, u32[]{:S(2)}, u32[]{:S(2)}) collective-permute-start(bf16[16,3072]{1,0:T(8,128)(2,1)S(1)} %bitcast.45), channel_id=1, source_target_pairs={{0,3},{1,2},{2,1},{3,0},{4,7},{5,6},{6,5},{7,4},{8,11},{9,10},{10,... | collective-permute-start | bytes 294920 | tf_op jit(solution)/shard_map/ppermute | solution.py:107
  38.5 2.5 %collective-permute-start.11 = (bf16[384,384]{1,0:T(8,128)(2,1)S(1)}, bf16[384,384]{1,0:T(8,128)(2,1)S(1)}, u32[]{:S(2)}, u32[]{:S(2)}) collective-permute-start(bf16[384,384]{1,0:T(8,128)(2,1)S(1)} %collective-permute-done.8.refs_2_), channel_id=1, source_target_pairs={{0,24},{1,25},{2,26},{3,27},{4,28},{5,29},{6,30},{7,31},{8,16},{9,... | collective-permute-start | bytes 884744 | tf_op jit(solution)/shard_map/ppermute | solution.py:107
  41.0 0.5 collective-permute-start.9
  41.5 1.5 %fusion.9.refs_1_ = bf16[128,3072]{1,0:T(8,128)(2,1)S(1)} fusion(bf16[128,3072]{1,0:T(8,128)(2,1)} %collective-permute-done, f32[128]{0:T(128)S(1)} %add_rsqrt_fusion, f32[128]{0:T(128)S(1)} %broadcast_multiply_fusion, f32[3072]{0:T(1024)S(1)} %bitcast.42, f32[3072]{0:T(1024)S(1)} %bitcast.40), kind=kLoop, calls=%fused_computation.14 | loop fusion | flops 2359296 | bytes 1598464 | tf_op jit(solution)/shard_map/convert_element_type | solution.py:28
  43.1 2.0 %shard_map.55 = (bf16[256,128]{1,0:T(8,128)(2,1)S(1)}, bf16[256,256]{1,0:T(8,128)(2,1)S(1)}) custom-call(s32[8]{0:T(128)S(1)} %stack.50.owner_ref, bf16[128,128]{1,0:T(8,128)(2,1)S(1)} %fusion.24.reorder_ref, bf16[128,3072]{1,0:T(8,128)(2,1)S(1)} %fusion.13.refs_0_, bf16[128,3072]{1,0:T(8,128)(2,1)S(1)} %fusion.9.refs_1_, bf16[384,384]{1,0:T(8,128)(2,1)S(1)} %bitcast.36, ...), custom_call_target="tpu_custom_call" | custom-call | flops 603979776 | bytes 3932160 | tf_op jit(solution)/shard_map/pallas_call | solution.py:64
  45.0 4.3 %collective-permute-done.11.refs_5_ = bf16[384,384]{1,0:T(8,128)(2,1)S(1)} collective-permute-done((bf16[384,384]{1,0:T(8,128)(2,1)S(1)}, bf16[384,384]{1,0:T(8,128)(2,1)S(1)}, u32[]{:S(2)}, u32[]{:S(2)}) %collective-permute-start.11) | collective-permute-done | bytes 294944 | tf_op jit(solution)/shard_map/ppermute | solution.py:107
  49.3 5.1 %collective-permute-done.9.refs_3_ = bf16[384,384]{1,0:T(8,128)(2,1)S(1)} collective-permute-done((bf16[384,384]{1,0:T(8,128)(2,1)S(1)}, bf16[384,384]{1,0:T(8,128)(2,1)S(1)}, u32[]{:S(2)}, u32[]{:S(2)}) %collective-permute-start.9) | collective-permute-done | bytes 294944 | tf_op jit(solution)/shard_map/ppermute | solution.py:107
  54.4 0.5 collective-permute-start.13
  54.9 0.5 collective-permute-start.15
  55.5 0.5 collective-permute-start.17
  56.0 1.6 %collective-permute-start.22 = (bf16[4,16,3072]{2,1,0:T(8,128)(2,1)S(1)}, bf16[4,16,3072]{2,1,0:T(8,128)(2,1)S(1)}, u32[]{:S(2)}, u32[]{:S(2)}) collective-permute-start(bf16[4,16,3072]{2,1,0:T(8,128)(2,1)S(1)} %pad_maximum_fusion), channel_id=1, source_target_pairs={{0,8},{1,9},{2,10},{3,11},{4,12},{5,13},{6,14},{7,15},{8,0},{9,1},... | collective-permute-start | bytes 1179656 | tf_op jit(solution)/shard_map/ppermute | solution.py:107
  57.6 0.5 collective-permute-start.23
  58.1 1.5 %collective-permute-start.24 = (bf16[4,16,3072]{2,1,0:T(8,128)(2,1)S(1)}, bf16[4,16,3072]{2,1,0:T(8,128)(2,1)S(1)}, u32[]{:S(2)}, u32[]{:S(2)}) collective-permute-start(bf16[4,16,3072]{2,1,0:T(8,128)(2,1)S(1)} %pad_maximum_fusion), channel_id=1, source_target_pairs={{0,24},{1,25},{2,26},{3,27},{4,28},{5,29},{6,30},{7,31},{8,16},{9,... | collective-permute-start | bytes 1179656 | tf_op jit(solution)/shard_map/ppermute | solution.py:107
  59.6 2.0 %shard_map.56 = (bf16[256,128]{1,0:T(8,128)(2,1)S(1)}, bf16[256,256]{1,0:T(8,128)(2,1)S(1)}) custom-call(s32[8]{0:T(128)S(1)} %stack.50.owner_ref, bf16[128,128]{1,0:T(8,128)(2,1)S(1)} %fusion.24.reorder_ref, bf16[128,3072]{1,0:T(8,128)(2,1)S(1)} %fusion.13.refs_0_, bf16[128,3072]{1,0:T(8,128)(2,1)S(1)} %fusion.9.refs_1_, ...), custom_call_target="tpu_custom_call" | custom-call | flops 603979776 | bytes 3932160 | tf_op jit(solution)/shard_map/pallas_call | solution.py:64
  61.6 2.5 %collective-permute-start.16 = (bf16[256,256]{1,0:T(8,128)(2,1)S(1)}, bf16[256,256]{1,0:T(8,128)(2,1)S(1)}, u32[]{:S(2)}, u32[]{:S(2)}) collective-permute-start(bf16[256,256]{1,0:T(8,128)(2,1)S(1)} %get-tuple-element.29), channel_id=1, source_target_pairs={{0,2},{1,3},{2,0},{3,1},{4,6},{5,7},{6,4},{7,5},{8,10},{9,11},{10,... | collective-permute-start | bytes 393224 | tf_op jit(solution)/shard_map/ppermute | solution.py:107
  64.1 0.7 collective-permute-done.17
  64.8 0.3 fusion.29
  65.1 0.2 fusion.15
  65.4 0.3 convolution_convert_fusion
  65.7 2.4 %collective-permute-done.22 = bf16[4,16,3072]{2,1,0:T(8,128)(2,1)S(1)} collective-permute-done((bf16[4,16,3072]{2,1,0:T(8,128)(2,1)S(1)}, bf16[4,16,3072]{2,1,0:T(8,128)(2,1)S(1)}, u32[]{:S(2)}, u32[]{:S(2)}) %collective-permute-start.22) | collective-permute-done | bytes 393248 | tf_op jit(solution)/shard_map/ppermute | solution.py:107
  68.1 8.7 %collective-permute-done.23 = bf16[4,16,3072]{2,1,0:T(8,128)(2,1)S(1)} collective-permute-done((bf16[4,16,3072]{2,1,0:T(8,128)(2,1)S(1)}, bf16[4,16,3072]{2,1,0:T(8,128)(2,1)S(1)}, u32[]{:S(2)}, u32[]{:S(2)}) %collective-permute-start.23) | collective-permute-done | bytes 393248 | tf_op jit(solution)/shard_map/ppermute | solution.py:107
  76.9 0.5 collective-permute-start.26
  77.4 0.1 collective-permute-start.27
  77.6 0.5 collective-permute-start.28
  78.2 0.3 fusion.28
  78.5 0.2 fusion.14
  78.7 0.3 convolution_convert_fusion.1
  79.1 2.4 %collective-permute-start.18 = (bf16[128,256]{0,1:T(8,128)(2,1)S(1)}, bf16[128,256]{0,1:T(8,128)(2,1)S(1)}, u32[]{:S(2)}, u32[]{:S(2)}) collective-permute-start(bf16[128,256]{0,1:T(8,128)(2,1)S(1)} %get-tuple-element.38), channel_id=1, source_target_pairs={{0,1},{1,0},{2,3},{3,2},{4,5},{5,4},{6,7},{7,6},{8,9},{9,8},{10,11... | collective-permute-start | bytes 196616 | tf_op jit(solution)/shard_map/ppermute | solution.py:107
  81.6 2.2 %collective-permute-done.18 = bf16[128,256]{0,1:T(8,128)(2,1)S(1)} collective-permute-done((bf16[128,256]{0,1:T(8,128)(2,1)S(1)}, bf16[128,256]{0,1:T(8,128)(2,1)S(1)}, u32[]{:S(2)}, u32[]{:S(2)}) %collective-permute-start.18) | collective-permute-done | bytes 65568 | tf_op jit(solution)/shard_map/ppermute | solution.py:107
  83.8 1.5 %fusion.1 = bf16[1,128,3072]{2,1,0:T(8,128)(2,1)} fusion(bf16[512,3072]{1,0:T(8,128)(2,1)S(1)} %bitcast.38, f32[3072]{0:T(1024)S(1)} %bitcast.49, bf16[128,256]{0,1:T(8,128)(2,1)S(1)} %collective-permute-done.18, bf16[128,256]{0,1:T(8,128)(2,1)S(1)} %get-tuple-element.37), kind=kOutput, calls=%fused_computation.2 | convolution fusion | flops 403701760 | bytes 4075520 | tf_op jit(solution)/shard_map/dot_general | solution.py:190
  (60 shorter events, 0.8 us)
Async XLA Ops:
  0.0 14.4 %copy-start.1 = (bf16[1,128,3072]{2,1,0:T(8,128)(2,1)S(1)}, bf16[1,128,3072]{2,1,0:T(8,128)(2,1)}, u32[]{:S(2)}) copy-start(bf16[1,128,3072]{2,1,0:T(8,128)(2,1)} %param.5) | copy-start | bytes 2359300
  0.0 20.4 %collective-permute-start.1 = (bf16[384,384]{1,0:T(8,128)(2,1)}, bf16[384,384]{1,0:T(8,128)(2,1)S(1)}, u32[]{:S(2)}, u32[]{:S(2)}) collective-permute-start(bf16[384,384]{1,0:T(8,128)(2,1)} %bitcast.31), channel_id=1, source_target_pairs={{0,8},{1,9},{2,10},{3,11},{4,12},{5,13},{6,14},{7,15},{8,0},{9,1},... | collective-permute-start | bytes 884744 | tf_op jit(solution)/shard_map/ppermute | solution.py:107
  3.0 19.1 %collective-permute-start.2 = (bf16[384,384]{1,0:T(8,128)(2,1)}, bf16[384,384]{1,0:T(8,128)(2,1)S(1)}, u32[]{:S(2)}, u32[]{:S(2)}) collective-permute-start(bf16[384,384]{1,0:T(8,128)(2,1)} %bitcast.32), channel_id=1, source_target_pairs={{0,16},{1,17},{2,18},{3,19},{4,20},{5,21},{6,22},{7,23},{8,24},{9,... | collective-permute-start | bytes 884744 | tf_op jit(solution)/shard_map/ppermute | solution.py:107
  4.5 17.7 %collective-permute-start.3 = (bf16[384,384]{1,0:T(8,128)(2,1)}, bf16[384,384]{1,0:T(8,128)(2,1)S(1)}, u32[]{:S(2)}, u32[]{:S(2)}) collective-permute-start(bf16[384,384]{1,0:T(8,128)(2,1)} %bitcast.33), channel_id=1, source_target_pairs={{0,24},{1,25},{2,26},{3,27},{4,28},{5,29},{6,30},{7,31},{8,16},{9,... | collective-permute-start | bytes 884744 | tf_op jit(solution)/shard_map/ppermute | solution.py:107
  4.5 15.9 %collective-permute-start.8 = (bf16[384,384]{1,0:T(8,128)(2,1)}, bf16[384,384]{1,0:T(8,128)(2,1)S(1)}, u32[]{:S(2)}, u32[]{:S(2)}) collective-permute-start(bf16[384,384]{1,0:T(8,128)(2,1)} %bitcast.34), channel_id=1, source_target_pairs={{0,2},{1,3},{2,0},{3,1},{4,6},{5,7},{6,4},{7,5},{8,10},{9,11},{10,... | collective-permute-start | bytes 884744 | tf_op jit(solution)/shard_map/ppermute | solution.py:107
  7.6 23.6 %collective-permute-start = (bf16[128,3072]{1,0:T(8,128)(2,1)}, bf16[128,3072]{1,0:T(8,128)(2,1)}, u32[]{:S(2)}, u32[]{:S(2)}) collective-permute-start(bf16[128,3072]{1,0:T(8,128)(2,1)} %bitcast.37), channel_id=1, source_target_pairs={{0,1},{1,0},{2,3},{3,2},{4,5},{5,4},{6,7},{7,6},{8,9},{9,8},{10,11... | collective-permute-start | bytes 2359304 | tf_op jit(solution)/shard_map/ppermute | solution.py:107
  11.2 9.2 %copy-start = (bf16[1,384,384]{2,1,0:T(8,128)(2,1)S(1)}, bf16[1,384,384]{2,1,0:T(8,128)(2,1)}, u32[]{:S(2)}) copy-start(bf16[1,384,384]{2,1,0:T(8,128)(2,1)} %param.8) | copy-start | bytes 884740
  14.3 19.7 %copy-start.2 = (bf16[1,16,3072]{2,1,0:T(8,128)(2,1)S(1)}, bf16[1,16,3072]{2,1,0:T(8,128)(2,1)}, u32[]{:S(2)}) copy-start(bf16[1,16,3072]{2,1,0:T(8,128)(2,1)} %param.9) | copy-start | bytes 294916
  20.4 13.6 %collective-permute-start.4 = (bf16[384,384]{1,0:T(8,128)(2,1)S(1)}, bf16[384,384]{1,0:T(8,128)(2,1)S(1)}, u32[]{:S(2)}, u32[]{:S(2)}) collective-permute-start(bf16[384,384]{1,0:T(8,128)(2,1)S(1)} %bitcast.35), channel_id=1, source_target_pairs={{0,4},{1,5},{2,6},{3,7},{4,0},{5,1},{6,2},{7,3},{8,12},{9,13},{10,... | collective-permute-start | bytes 884744 | tf_op jit(solution)/shard_map/ppermute | solution.py:107
  20.4 20.6 %collective-permute-start.10 = (bf16[384,384]{1,0:T(8,128)(2,1)S(1)}, bf16[384,384]{1,0:T(8,128)(2,1)S(1)}, u32[]{:S(2)}, u32[]{:S(2)}) collective-permute-start(bf16[384,384]{1,0:T(8,128)(2,1)S(1)} %collective-permute-done.8.refs_2_), channel_id=1, source_target_pairs={{0,16},{1,17},{2,18},{3,19},{4,20},{5,21},{6,22},{7,23},{8,24},{9,... | collective-permute-start | bytes 884744 | tf_op jit(solution)/shard_map/ppermute | solution.py:107
  22.0 13.5 %collective-permute-start.5 = (bf16[384,384]{1,0:T(8,128)(2,1)S(1)}, bf16[384,384]{1,0:T(8,128)(2,1)S(1)}, u32[]{:S(2)}, u32[]{:S(2)}) collective-permute-start(bf16[384,384]{1,0:T(8,128)(2,1)S(1)} %collective-permute-done.1.refs_3_), channel_id=1, source_target_pairs={{0,4},{1,5},{2,6},{3,7},{4,0},{5,1},{6,2},{7,3},{8,12},{9,13},{10,... | collective-permute-start | bytes 884744 | tf_op jit(solution)/shard_map/ppermute | solution.py:107
  22.2 15.0 %collective-permute-start.6 = (bf16[384,384]{1,0:T(8,128)(2,1)S(1)}, bf16[384,384]{1,0:T(8,128)(2,1)S(1)}, u32[]{:S(2)}, u32[]{:S(2)}) collective-permute-start(bf16[384,384]{1,0:T(8,128)(2,1)S(1)} %collective-permute-done.2.refs_4_), channel_id=1, source_target_pairs={{0,4},{1,5},{2,6},{3,7},{4,0},{5,1},{6,2},{7,3},{8,12},{9,13},{10,... | collective-permute-start | bytes 884744 | tf_op jit(solution)/shard_map/ppermute | solution.py:107
  31.2 7.3 %collective-permute-start.7 = (bf16[384,384]{1,0:T(8,128)(2,1)S(1)}, bf16[384,384]{1,0:T(8,128)(2,1)S(1)}, u32[]{:S(2)}, u32[]{:S(2)}) collective-permute-start(bf16[384,384]{1,0:T(8,128)(2,1)S(1)} %collective-permute-done.3.refs_5_), channel_id=1, source_target_pairs={{0,4},{1,5},{2,6},{3,7},{4,0},{5,1},{6,2},{7,3},{8,12},{9,13},{10,... | collective-permute-start | bytes 884744 | tf_op jit(solution)/shard_map/ppermute | solution.py:107
  34.1 20.9 %collective-permute-start.19 = (bf16[16,3072]{1,0:T(8,128)(2,1)S(1)}, bf16[16,3072]{1,0:T(8,128)(2,1)S(1)}, u32[]{:S(2)}, u32[]{:S(2)}) collective-permute-start(bf16[16,3072]{1,0:T(8,128)(2,1)S(1)} %bitcast.43), channel_id=1, source_target_pairs={{0,2},{1,3},{2,0},{3,1},{4,6},{5,7},{6,4},{7,5},{8,10},{9,11},{10,... | collective-permute-start | bytes 294920 | tf_op jit(solution)/shard_map/ppermute | solution.py:107
  35.5 19.4 %collective-permute-start.20 = (bf16[16,3072]{1,0:T(8,128)(2,1)S(1)}, bf16[16,3072]{1,0:T(8,128)(2,1)S(1)}, u32[]{:S(2)}, u32[]{:S(2)}) collective-permute-start(bf16[16,3072]{1,0:T(8,128)(2,1)S(1)} %bitcast.44), channel_id=1, source_target_pairs={{0,1},{1,0},{2,3},{3,2},{4,5},{5,4},{6,7},{7,6},{8,9},{9,8},{10,11... | collective-permute-start | bytes 294920 | tf_op jit(solution)/shard_map/ppermute | solution.py:107
  37.2 18.3 %collective-permute-start.21 = (bf16[16,3072]{1,0:T(8,128)(2,1)S(1)}, bf16[16,3072]{1,0:T(8,128)(2,1)S(1)}, u32[]{:S(2)}, u32[]{:S(2)}) collective-permute-start(bf16[16,3072]{1,0:T(8,128)(2,1)S(1)} %bitcast.45), channel_id=1, source_target_pairs={{0,3},{1,2},{2,1},{3,0},{4,7},{5,6},{6,5},{7,4},{8,11},{9,10},{10,... | collective-permute-start | bytes 294920 | tf_op jit(solution)/shard_map/ppermute | solution.py:107
  38.5 10.8 %collective-permute-start.11 = (bf16[384,384]{1,0:T(8,128)(2,1)S(1)}, bf16[384,384]{1,0:T(8,128)(2,1)S(1)}, u32[]{:S(2)}, u32[]{:S(2)}) collective-permute-start(bf16[384,384]{1,0:T(8,128)(2,1)S(1)} %collective-permute-done.8.refs_2_), channel_id=1, source_target_pairs={{0,24},{1,25},{2,26},{3,27},{4,28},{5,29},{6,30},{7,31},{8,16},{9,... | collective-permute-start | bytes 884744 | tf_op jit(solution)/shard_map/ppermute | solution.py:107
  41.0 13.4 %collective-permute-start.9 = (bf16[384,384]{1,0:T(8,128)(2,1)S(1)}, bf16[384,384]{1,0:T(8,128)(2,1)S(1)}, u32[]{:S(2)}, u32[]{:S(2)}) collective-permute-start(bf16[384,384]{1,0:T(8,128)(2,1)S(1)} %collective-permute-done.8.refs_2_), channel_id=1, source_target_pairs={{0,8},{1,9},{2,10},{3,11},{4,12},{5,13},{6,14},{7,15},{8,0},{9,1},... | collective-permute-start | bytes 884744 | tf_op jit(solution)/shard_map/ppermute | solution.py:107
  54.4 1.6 %collective-permute-start.12 = (bf16[384,384]{1,0:T(8,128)(2,1)S(1)}, bf16[384,384]{1,0:T(8,128)(2,1)S(1)}, u32[]{:S(2)}, u32[]{:S(2)}) collective-permute-start(bf16[384,384]{1,0:T(8,128)(2,1)S(1)} %collective-permute-done.8.refs_2_), channel_id=1, source_target_pairs={{0,4},{1,5},{2,6},{3,7},{4,0},{5,1},{6,2},{7,3},{8,12},{9,13},{10,... | collective-permute-start | bytes 884744 | tf_op jit(solution)/shard_map/ppermute | solution.py:107
  54.4 3.2 %collective-permute-start.13 = (bf16[384,384]{1,0:T(8,128)(2,1)S(1)}, bf16[384,384]{1,0:T(8,128)(2,1)S(1)}, u32[]{:S(2)}, u32[]{:S(2)}) collective-permute-start(bf16[384,384]{1,0:T(8,128)(2,1)S(1)} %collective-permute-done.9.refs_3_), channel_id=1, source_target_pairs={{0,4},{1,5},{2,6},{3,7},{4,0},{5,1},{6,2},{7,3},{8,12},{9,13},{10,... | collective-permute-start | bytes 884744 | tf_op jit(solution)/shard_map/ppermute | solution.py:107
  54.9 3.2 %collective-permute-start.14 = (bf16[384,384]{1,0:T(8,128)(2,1)S(1)}, bf16[384,384]{1,0:T(8,128)(2,1)S(1)}, u32[]{:S(2)}, u32[]{:S(2)}) collective-permute-start(bf16[384,384]{1,0:T(8,128)(2,1)S(1)} %collective-permute-done.10.refs_4_), channel_id=1, source_target_pairs={{0,4},{1,5},{2,6},{3,7},{4,0},{5,1},{6,2},{7,3},{8,12},{9,13},{10,... | collective-permute-start | bytes 884744 | tf_op jit(solution)/shard_map/ppermute | solution.py:107
  54.9 4.7 %collective-permute-start.15 = (bf16[384,384]{1,0:T(8,128)(2,1)S(1)}, bf16[384,384]{1,0:T(8,128)(2,1)S(1)}, u32[]{:S(2)}, u32[]{:S(2)}) collective-permute-start(bf16[384,384]{1,0:T(8,128)(2,1)S(1)} %collective-permute-done.11.refs_5_), channel_id=1, source_target_pairs={{0,4},{1,5},{2,6},{3,7},{4,0},{5,1},{6,2},{7,3},{8,12},{9,13},{10,... | collective-permute-start | bytes 884744 | tf_op jit(solution)/shard_map/ppermute | solution.py:107
  55.5 9.3 %collective-permute-start.17 = (bf16[256,256]{1,0:T(8,128)(2,1)S(1)}, bf16[256,256]{1,0:T(8,128)(2,1)S(1)}, u32[]{:S(2)}, u32[]{:S(2)}) collective-permute-start(bf16[256,256]{1,0:T(8,128)(2,1)S(1)} %get-tuple-element.23), channel_id=1, source_target_pairs={{0,2},{1,3},{2,0},{3,1},{4,6},{5,7},{6,4},{7,5},{8,10},{9,11},{10,... | collective-permute-start | bytes 393224 | tf_op jit(solution)/shard_map/ppermute | solution.py:107
  56.0 12.1 %collective-permute-start.22 = (bf16[4,16,3072]{2,1,0:T(8,128)(2,1)S(1)}, bf16[4,16,3072]{2,1,0:T(8,128)(2,1)S(1)}, u32[]{:S(2)}, u32[]{:S(2)}) collective-permute-start(bf16[4,16,3072]{2,1,0:T(8,128)(2,1)S(1)} %pad_maximum_fusion), channel_id=1, source_target_pairs={{0,8},{1,9},{2,10},{3,11},{4,12},{5,13},{6,14},{7,15},{8,0},{9,1},... | collective-permute-start | bytes 1179656 | tf_op jit(solution)/shard_map/ppermute | solution.py:107
  57.6 19.2 %collective-permute-start.23 = (bf16[4,16,3072]{2,1,0:T(8,128)(2,1)S(1)}, bf16[4,16,3072]{2,1,0:T(8,128)(2,1)S(1)}, u32[]{:S(2)}, u32[]{:S(2)}) collective-permute-start(bf16[4,16,3072]{2,1,0:T(8,128)(2,1)S(1)} %pad_maximum_fusion), channel_id=1, source_target_pairs={{0,16},{1,17},{2,18},{3,19},{4,20},{5,21},{6,22},{7,23},{8,24},{9,... | collective-permute-start | bytes 1179656 | tf_op jit(solution)/shard_map/ppermute | solution.py:107
  58.1 18.7 %collective-permute-start.24 = (bf16[4,16,3072]{2,1,0:T(8,128)(2,1)S(1)}, bf16[4,16,3072]{2,1,0:T(8,128)(2,1)S(1)}, u32[]{:S(2)}, u32[]{:S(2)}) collective-permute-start(bf16[4,16,3072]{2,1,0:T(8,128)(2,1)S(1)} %pad_maximum_fusion), channel_id=1, source_target_pairs={{0,24},{1,25},{2,26},{3,27},{4,28},{5,29},{6,30},{7,31},{8,16},{9,... | collective-permute-start | bytes 1179656 | tf_op jit(solution)/shard_map/ppermute | solution.py:107
  61.6 16.6 %collective-permute-start.16 = (bf16[256,256]{1,0:T(8,128)(2,1)S(1)}, bf16[256,256]{1,0:T(8,128)(2,1)S(1)}, u32[]{:S(2)}, u32[]{:S(2)}) collective-permute-start(bf16[256,256]{1,0:T(8,128)(2,1)S(1)} %get-tuple-element.29), channel_id=1, source_target_pairs={{0,2},{1,3},{2,0},{3,1},{4,6},{5,7},{6,4},{7,5},{8,10},{9,11},{10,... | collective-permute-start | bytes 393224 | tf_op jit(solution)/shard_map/ppermute | solution.py:107
  76.8 4.6 %collective-permute-start.25 = (bf16[4,16,3072]{2,1,0:T(8,128)(2,1)S(1)}, bf16[4,16,3072]{2,1,0:T(8,128)(2,1)S(1)}, u32[]{:S(2)}, u32[]{:S(2)}) collective-permute-start(bf16[4,16,3072]{2,1,0:T(8,128)(2,1)S(1)} %pad_maximum_fusion), channel_id=1, source_target_pairs={{0,4},{1,5},{2,6},{3,7},{4,0},{5,1},{6,2},{7,3},{8,12},{9,13},{10,... | collective-permute-start | bytes 1179656 | tf_op jit(solution)/shard_map/ppermute | solution.py:107
  76.9 4.6 %collective-permute-start.26 = (bf16[4,16,3072]{2,1,0:T(8,128)(2,1)S(1)}, bf16[4,16,3072]{2,1,0:T(8,128)(2,1)S(1)}, u32[]{:S(2)}, u32[]{:S(2)}) collective-permute-start(bf16[4,16,3072]{2,1,0:T(8,128)(2,1)S(1)} %collective-permute-done.22), channel_id=1, source_target_pairs={{0,4},{1,5},{2,6},{3,7},{4,0},{5,1},{6,2},{7,3},{8,12},{9,13},{10,... | collective-permute-start | bytes 1179656 | tf_op jit(solution)/shard_map/ppermute | solution.py:107
  77.4 4.1 %collective-permute-start.27 = (bf16[4,16,3072]{2,1,0:T(8,128)(2,1)S(1)}, bf16[4,16,3072]{2,1,0:T(8,128)(2,1)S(1)}, u32[]{:S(2)}, u32[]{:S(2)}) collective-permute-start(bf16[4,16,3072]{2,1,0:T(8,128)(2,1)S(1)} %collective-permute-done.23), channel_id=1, source_target_pairs={{0,4},{1,5},{2,6},{3,7},{4,0},{5,1},{6,2},{7,3},{8,12},{9,13},{10,... | collective-permute-start | bytes 1179656 | tf_op jit(solution)/shard_map/ppermute | solution.py:107
  77.6 4.0 %collective-permute-start.28 = (bf16[4,16,3072]{2,1,0:T(8,128)(2,1)S(1)}, bf16[4,16,3072]{2,1,0:T(8,128)(2,1)S(1)}, u32[]{:S(2)}, u32[]{:S(2)}) collective-permute-start(bf16[4,16,3072]{2,1,0:T(8,128)(2,1)S(1)} %collective-permute-done.24), channel_id=1, source_target_pairs={{0,4},{1,5},{2,6},{3,7},{4,0},{5,1},{6,2},{7,3},{8,12},{9,13},{10,... | collective-permute-start | bytes 1179656 | tf_op jit(solution)/shard_map/ppermute | solution.py:107
  79.1 4.7 %collective-permute-start.18 = (bf16[128,256]{0,1:T(8,128)(2,1)S(1)}, bf16[128,256]{0,1:T(8,128)(2,1)S(1)}, u32[]{:S(2)}, u32[]{:S(2)}) collective-permute-start(bf16[128,256]{0,1:T(8,128)(2,1)S(1)} %get-tuple-element.38), channel_id=1, source_target_pairs={{0,1},{1,0},{2,3},{3,2},{4,5},{5,4},{6,7},{7,6},{8,9},{9,8},{10,11... | collective-permute-start | bytes 196616 | tf_op jit(solution)/shard_map/ppermute | solution.py:107
where the time goes:
time: 85.6 us; the launch traced here: 85.3 us
  waiting for transfers between devices  36.9 us (43%)
  starting transfers between devices  30 us (35%)
  other arithmetic  7.1 us (8%)
  matrix products  5.86 us (7%)
  Pallas kernels  3.92 us (5%)
  between operations  0.98 us (1%)
    ppermute x29, waiting for transfers between devices, move(): return lax.ppermute(value, AXES, pairs)  36.9 us
    ppermute x29, starting transfers between devices, move(): return lax.ppermute(value, AXES, pairs)  30 us
    pallas_call x2, Pallas kernels, project(): pl.pallas_call(functools.partial(project_kernel, len(xs)), out_shape=(jax...  3.92 us
    dot_general x1, matrix products, modulation(): return jnp.dot(embed, w_mod, preferred_element_type=jnp.float32)  3.1 us
    reduce_sum x2, other arithmetic, normalize(): center = jnp.mean(values, axis=-1, keepdims=True)  2.68 us
    convert_element_type x2, other arithmetic, normalize(): return (normed * (1.0 + scale) + shift).astype(jnp.bfloat16)  1.91 us
    reduce_sum x2, other arithmetic, normalize(): spread = jnp.mean((values - center) ** 2, axis=-1, keepdims=True)  1.85 us
  transfers between devices with their start and end apart: 29, of which 8 were waited for; matrix products, arithmetic and copies ran while one was open for 14% of the time, Pallas kernels for 5%

commit v1 on v0

--- a/solution.py
+++ b/solution.py
@@ -20,12 +20,32 @@
     return jnp.dot(embed, w_mod, preferred_element_type=jnp.float32)
 
 
-def normalize(latents, shift, scale):
-    values = latents.astype(jnp.float32)
-    center = jnp.mean(values, axis=-1, keepdims=True)
-    spread = jnp.mean((values - center) ** 2, axis=-1, keepdims=True)
-    normed = (values - center) * lax.rsqrt(spread + 1e-06)
-    return (normed * (1.0 + scale) + shift).astype(jnp.bfloat16)
+def normalize_kernel(block, x_ref, shift_ref, scale_ref, out_ref):
+    gain = 1.0 + scale_ref[...]
+    shift = shift_ref[...]
+
+    @pl.loop(0, x_ref.shape[0] // block)
+    def _(step):
+        rows = pl.ds(pl.multiple_of(step * block, block), block)
+        values = x_ref[rows, :].astype(jnp.float32)
+        centered = values - jnp.mean(values, axis=-1, keepdims=True)
+        spread = jnp.mean(centered * centered, axis=-1, keepdims=True)
+        out_ref[rows, :] = (centered * lax.rsqrt(spread + 1e-06) * gain + shift).astype(out_ref.dtype)
+
+
+def normalize(rows, shift, scale):
+    vmem = pl.BlockSpec(memory_space=pltpu.VMEM)
+    block = math.gcd(rows.shape[0], 32)
+    return pl.pallas_call(
+        functools.partial(normalize_kernel, block),
+        out_shape=jax.ShapeDtypeStruct(rows.shape, jnp.bfloat16),
+        in_specs=[vmem] * 3,
+        out_specs=vmem,
+        compiler_params=pltpu.CompilerParams(vmem_limit_bytes=8 * 2**20),
+        cost_estimate=pl.CostEstimate(
+            flops=10 * rows.size, bytes_accessed=4 * rows.size, transcendentals=0
+        ),
+    )(rows, shift, scale)
 
 
 def project_kernel(chunks, owner_ref, reorder_ref, *refs):
@@ -161,17 +181,15 @@
 
     xs = [mine_normed] + [normalize(rows, shift, scale) for rows in after(raw, mine_normed)[1:]]
 
-    queries, local_kv, remote_kv = [], [], []
-    for pieces in (own_pieces, None):
-        if pieces is None:
-            other_in = after(other_in, local_kv[0])
-            out_mine = over_chips(after(jnp.stack(out_shards), local_kv[0]))
-            pieces = over_cores(other_in)
-        query, kv = project(xs, pieces, owners, reorder)
-        queries.append(query)
-        local_kv.append(kv)
-        remote_kv.append(move(kv, same, sp_shift(1, 0)))
-    out_pieces = over_cores(after(out_mine, local_kv[1]))
+    query_0, kv_0 = project(xs, own_pieces, owners, reorder)
+    remote_0 = move(kv_0, same, sp_shift(1, 0))
+    out_mine = over_chips(after(jnp.stack(out_shards), kv_0))
+    other_in = after(other_in, kv_0)
+    other_pieces = over_cores(other_in)
+    query_1, kv_1 = project(xs, other_pieces, owners, reorder)
+    remote_1 = move(kv_1, same, sp_shift(1, 0))
+    out_pieces = over_cores(after(out_mine, kv_1))
+    queries, local_kv, remote_kv = [query_0, query_1], [kv_0, kv_1], [remote_0, remote_1]
 
     heads = [None, None]
     for index in (1, 0):

time: 85.6 us -> 79.4 us (0.928)
  other arithmetic: 7.1 us -> 1.17 us
  waiting for transfers between devices: 36.9 us -> 32.4 us
  local copies, waits for them, and re-layouts: 0.51 us -> 4.26 us
  Pallas kernels: 3.92 us -> 7.36 us
  starting transfers between devices: 30 us -> 27.1 us
    ppermute x29, waiting for transfers between devices: 36.9 us -> 32.4 us  [move(): return lax.ppermute(value, AXES, pairs)]
    reduce_sum x4 -> x0, other arithmetic: 4.53 us -> none  [the longest x2 2.68 us: normalize(): center = jnp.mean(values, axis=-1, keepdims=True)]
    ppermute x29, starting transfers between devices: 30 us -> 27.1 us  [move(): return lax.ppermute(value, AXES, pairs)]
    pallas_call x0 -> x2, Pallas kernels: none -> 2.26 us  [normalize(): pl.pallas_call(functools.partial(normalize_kernel, block), out_shape=jax....]
    convert_element_type x2 -> x0, other arithmetic: 1.91 us -> none  [normalize(): return (normed * (1.0 + scale) + shift).astype(jnp.bfloat16)]
    unnamed x15 -> x21, local copies, waits for them, and re-layouts: 0.22 us -> 1.63 us
    pallas_call x2, Pallas kernels: 3.92 us -> 5.1 us  [project(): pl.pallas_call(functools.partial(project_kernel, len(xs)), out_shape=(jax...]
    mul x1, local copies, waits for them, and re-layouts: 0.08 us -> 1.23 us  [on_device(): source = jnp.repeat(owners, rows_each) * rows_each + column % rows_each]
  transfers between devices with their start and end apart: 29 -> 29, of which waited for: 8 -> 7; matrix products, arithmetic and copies ran while one was open for 14% -> 11% of each run, Pallas kernels for 5% -> 9%
where the time goes in v1:
time: 79.4 us; the launch traced here: 79.1 us
  waiting for transfers between devices  32.4 us (41%)
  starting transfers between devices  27.1 us (34%)
  Pallas kernels  7.36 us (9%)
  matrix products  5.86 us (7%)
  local copies, waits for them, and re-layouts  4.26 us (5%)
  other arithmetic  1.17 us (1%)
  between operations  0.94 us (1%)
    ppermute x29, waiting for transfers between devices, move(): return lax.ppermute(value, AXES, pairs)  32.4 us
    ppermute x29, starting transfers between devices, move(): return lax.ppermute(value, AXES, pairs)  27.1 us
    pallas_call x2, Pallas kernels, project(): pl.pallas_call(functools.partial(project_kernel, len(xs)), out_shape=(jax...  5.1 us
    dot_general x1, matrix products, modulation(): return jnp.dot(embed, w_mod, preferred_element_type=jnp.float32)  3.1 us
    pallas_call x2, Pallas kernels, normalize(): pl.pallas_call(functools.partial(normalize_kernel, block), out_shape=jax....  2.26 us
    unnamed x21, local copies, waits for them, and re-layouts  1.63 us
  transfers between devices with their start and end apart: 29, of which 7 were waited for; matrix products, arithmetic and copies ran while one was open for 11% of the time, Pallas kernels for 9%

profile of v1, /device:TPU:0, one launch (start us, length us, event | category | flops | bytes accessed | tf_op | source)
XLA Modules:
  0.0 79.1 jit_solution(6448286707717716924)
XLA Ops:
  0.0 3.0 %collective-permute-start.1 = (bf16[384,384]{1,0:T(8,128)(2,1)}, bf16[384,384]{1,0:T(8,128)(2,1)S(1)}, u32[]{:S(2)}, u32[]{:S(2)}) collective-permute-start(bf16[384,384]{1,0:T(8,128)(2,1)} %bitcast.28), channel_id=1, source_target_pairs={{0,8},{1,9},{2,10},{3,11},{4,12},{5,13},{6,14},{7,15},{8,0},{9,1},... | collective-permute-start | bytes 884744 | tf_op jit(solution)/shard_map/ppermute | solution.py:127
  3.0 1.5 %collective-permute-start.2 = (bf16[384,384]{1,0:T(8,128)(2,1)}, bf16[384,384]{1,0:T(8,128)(2,1)S(1)}, u32[]{:S(2)}, u32[]{:S(2)}) collective-permute-start(bf16[384,384]{1,0:T(8,128)(2,1)} %bitcast.29), channel_id=1, source_target_pairs={{0,16},{1,17},{2,18},{3,19},{4,20},{5,21},{6,22},{7,23},{8,24},{9,... | collective-permute-start | bytes 884744 | tf_op jit(solution)/shard_map/ppermute | solution.py:127
  4.5 3.1 %collective-permute-start.8 = (bf16[384,384]{1,0:T(8,128)(2,1)}, bf16[384,384]{1,0:T(8,128)(2,1)S(1)}, u32[]{:S(2)}, u32[]{:S(2)}) collective-permute-start(bf16[384,384]{1,0:T(8,128)(2,1)} %bitcast.32), channel_id=1, source_target_pairs={{0,2},{1,3},{2,0},{3,1},{4,6},{5,7},{6,4},{7,5},{8,10},{9,11},{10,... | collective-permute-start | bytes 884744 | tf_op jit(solution)/shard_map/ppermute | solution.py:127
  8.3 3.1 %fusion.18 = f32[1,9216]{1,0:T(1,128)S(1)} fusion(bf16[256,1]{0,1:T(2,128)(2,1)S(1)} %reshape.45, bf16[256,9216]{1,0:T(8,128)(2,1)} %param.7), kind=kOutput, calls=%fused_computation.50 | convolution fusion | flops 4718592 | bytes 4755968 | tf_op jit(solution)/shard_map/dot_general | solution.py:20
  11.4 1.7 %collective-permute-start = (bf16[128,3072]{1,0:T(8,128)(2,1)S(1)}, bf16[128,3072]{1,0:T(8,128)(2,1)S(1)}, u32[]{:S(2)}, u32[]{:S(2)}) collective-permute-start(bf16[128,3072]{1,0:T(8,128)(2,1)S(1)} %bitcast.26), channel_id=1, source_target_pairs={{0,1},{1,0},{2,3},{3,2},{4,5},{5,4},{6,7},{7,6},{8,9},{9,8},{10,11... | collective-permute-start | bytes 2359304 | tf_op jit(solution)/shard_map/ppermute | solution.py:127
  13.1 4.8 %collective-permute-done.2.refs_4_ = bf16[384,384]{1,0:T(8,128)(2,1)S(1)} collective-permute-done((bf16[384,384]{1,0:T(8,128)(2,1)}, bf16[384,384]{1,0:T(8,128)(2,1)S(1)}, u32[]{:S(2)}, u32[]{:S(2)}) %collective-permute-start.2) | collective-permute-done | bytes 294944 | tf_op jit(solution)/shard_map/ppermute | solution.py:127
  18.0 3.9 %collective-permute-done.8.refs_2_ = bf16[384,384]{1,0:T(8,128)(2,1)S(1)} collective-permute-done((bf16[384,384]{1,0:T(8,128)(2,1)}, bf16[384,384]{1,0:T(8,128)(2,1)S(1)}, u32[]{:S(2)}, u32[]{:S(2)}) %collective-permute-start.8) | collective-permute-done | bytes 294944 | tf_op jit(solution)/shard_map/ppermute | solution.py:127
  21.9 0.6 fusion.15
  22.5 0.1 stack.50.owner_ref
  22.6 0.7 copy-done.2
  23.3 1.1 %shard_map.55.refs_0_ = bf16[128,3072]{1,0:T(8,128)(2,1)S(1)} custom-call(bf16[128,3072]{1,0:T(8,128)(2,1)S(1)} %bitcast.27, f32[1,3072]{1,0:T(1,128)S(1)} %get-tuple-element.40.shift_ref, f32[1,3072]{1,0:T(1,128)S(1)} %copy-done.2), custom_call_target="tpu_custom_call" | custom-call | flops 3932160 | bytes 1572864 | tf_op jit(solution)/shard_map/pallas_call | solution.py:39
  24.4 1.6 %collective-permute-start.10 = (bf16[384,384]{1,0:T(8,128)(2,1)S(1)}, bf16[384,384]{1,0:T(8,128)(2,1)}, u32[]{:S(2)}, u32[]{:S(2)}) collective-permute-start(bf16[384,384]{1,0:T(8,128)(2,1)S(1)} %collective-permute-done.8.refs_2_), channel_id=1, source_target_pairs={{0,16},{1,17},{2,18},{3,19},{4,20},{5,21},{6,22},{7,23},{8,24},{9,... | collective-permute-start | bytes 884744 | tf_op jit(solution)/shard_map/ppermute | solution.py:127
  26.1 0.2 collective-permute-start.7
  26.3 0.7 broadcast_in_dim.4
  27.0 1.2 %mul.74 = s32[128]{0:T(128)} reshape(s32[8,16]{1,0:T(8,128)} %broadcast_in_dim.4) | data formatting | bytes 1024 | tf_op jit(solution)/shard_map/mul | solution.py:160
  28.2 1.4 %collective-permute-start.11 = (bf16[384,384]{1,0:T(8,128)(2,1)S(1)}, bf16[384,384]{1,0:T(8,128)(2,1)S(1)}, u32[]{:S(2)}, u32[]{:S(2)}) collective-permute-start(bf16[384,384]{1,0:T(8,128)(2,1)S(1)} %collective-permute-done.8.refs_2_), channel_id=1, source_target_pairs={{0,24},{1,25},{2,26},{3,27},{4,28},{5,29},{6,30},{7,31},{8,16},{9,... | collective-permute-start | bytes 884744 | tf_op jit(solution)/shard_map/ppermute | solution.py:127
  29.6 0.5 collective-permute-start.9
  30.1 0.6 fusion.13
  30.7 9.6 %collective-permute-done.10.refs_4_ = bf16[384,384]{1,0:T(8,128)(2,1)} collective-permute-done((bf16[384,384]{1,0:T(8,128)(2,1)S(1)}, bf16[384,384]{1,0:T(8,128)(2,1)}, u32[]{:S(2)}, u32[]{:S(2)}) %collective-permute-start.10) | collective-permute-done | bytes 294944 | tf_op jit(solution)/shard_map/ppermute | solution.py:127
  40.3 0.8 collective-permute-start.20
  41.1 2.8 %collective-permute-start.21 = (bf16[16,3072]{1,0:T(8,128)(2,1)}, bf16[16,3072]{1,0:T(8,128)(2,1)S(1)}, u32[]{:S(2)}, u32[]{:S(2)}) collective-permute-start(bf16[16,3072]{1,0:T(8,128)(2,1)} %bitcast.37), channel_id=1, source_target_pairs={{0,3},{1,2},{2,1},{3,0},{4,7},{5,6},{6,5},{7,4},{8,11},{9,10},{10,... | collective-permute-start | bytes 294920 | tf_op jit(solution)/shard_map/ppermute | solution.py:127
  43.9 0.7 copy-done.3
  44.6 1.1 %shard_map.56.refs_1_ = bf16[128,3072]{1,0:T(8,128)(2,1)S(1)} custom-call(bf16[128,3072]{1,0:T(8,128)(2,1)S(1)} %collective-permute-done.x_ref, f32[1,3072]{1,0:T(1,128)S(1)} %get-tuple-element.40.shift_ref, f32[1,3072]{1,0:T(1,128)S(1)} %copy-done.3), custom_call_target="tpu_custom_call" | custom-call | flops 3932160 | bytes 1572864 | tf_op jit(solution)/shard_map/pallas_call | solution.py:39
  45.8 2.7 %shard_map.57 = (bf16[256,128]{1,0:T(8,128)(2,1)S(1)}, bf16[256,256]{1,0:T(8,128)(2,1)S(1)}) custom-call(s32[8]{0:T(128)S(1)} %stack.50.owner_ref, bf16[128,128]{1,0:T(8,128)(2,1)S(1)} %fusion.12.reorder_ref, bf16[128,3072]{1,0:T(8,128)(2,1)S(1)} %shard_map.55.refs_0_, bf16[128,3072]{1,0:T(8,128)(2,1)S(1)} %shard_map.56.refs_1_, ...), custom_call_target="tpu_custom_call" | custom-call | flops 603979776 | bytes 3932160 | tf_op jit(solution)/shard_map/pallas_call | solution.py:84
  48.6 0.5 collective-permute-start.13
  49.1 0.1 collective-permute-start.14
  49.2 0.4 collective-permute-start.15
  49.7 1.3 %collective-permute-start.17 = (bf16[256,256]{1,0:T(8,128)(2,1)S(1)}, bf16[256,256]{1,0:T(8,128)(2,1)S(1)}, u32[]{:S(2)}, u32[]{:S(2)}) collective-permute-start(bf16[256,256]{1,0:T(8,128)(2,1)S(1)} %get-tuple-element.23), channel_id=1, source_target_pairs={{0,2},{1,3},{2,0},{3,1},{4,6},{5,7},{6,4},{7,5},{8,10},{9,11},{10,... | collective-permute-start | bytes 393224 | tf_op jit(solution)/shard_map/ppermute | solution.py:127
  51.0 1.6 %collective-permute-start.22 = (bf16[4,16,3072]{2,1,0:T(8,128)(2,1)S(1)}, bf16[4,16,3072]{2,1,0:T(8,128)(2,1)S(1)}, u32[]{:S(2)}, u32[]{:S(2)}) collective-permute-start(bf16[4,16,3072]{2,1,0:T(8,128)(2,1)S(1)} %pad_maximum_fusion), channel_id=1, source_target_pairs={{0,8},{1,9},{2,10},{3,11},{4,12},{5,13},{6,14},{7,15},{8,0},{9,1},... | collective-permute-start | bytes 1179656 | tf_op jit(solution)/shard_map/ppermute | solution.py:127
  52.5 1.5 %collective-permute-start.23 = (bf16[4,16,3072]{2,1,0:T(8,128)(2,1)S(1)}, bf16[4,16,3072]{2,1,0:T(8,128)(2,1)S(1)}, u32[]{:S(2)}, u32[]{:S(2)}) collective-permute-start(bf16[4,16,3072]{2,1,0:T(8,128)(2,1)S(1)} %pad_maximum_fusion), channel_id=1, source_target_pairs={{0,16},{1,17},{2,18},{3,19},{4,20},{5,21},{6,22},{7,23},{8,24},{9,... | collective-permute-start | bytes 1179656 | tf_op jit(solution)/shard_map/ppermute | solution.py:127
  54.1 0.5 collective-permute-start.24
  54.5 2.4 %shard_map.58 = (bf16[256,128]{1,0:T(8,128)(2,1)S(1)}, bf16[256,256]{1,0:T(8,128)(2,1)S(1)}) custom-call(s32[8]{0:T(128)S(1)} %stack.50.owner_ref, bf16[128,128]{1,0:T(8,128)(2,1)S(1)} %fusion.12.reorder_ref, bf16[128,3072]{1,0:T(8,128)(2,1)S(1)} %shard_map.55.refs_0_, bf16[128,3072]{1,0:T(8,128)(2,1)S(1)} %shard_map.56.refs_1_, ...), custom_call_target="tpu_custom_call" | custom-call | flops 603979776 | bytes 3932160 | tf_op jit(solution)/shard_map/pallas_call | solution.py:84
  56.9 1.8 %collective-permute-start.16 = (bf16[256,256]{1,0:T(8,128)(2,1)S(1)}, bf16[256,256]{1,0:T(8,128)(2,1)S(1)}, u32[]{:S(2)}, u32[]{:S(2)}) collective-permute-start(bf16[256,256]{1,0:T(8,128)(2,1)S(1)} %get-tuple-element.29), channel_id=1, source_target_pairs={{0,2},{1,3},{2,0},{3,1},{4,6},{5,7},{6,4},{7,5},{8,10},{9,11},{10,... | collective-permute-start | bytes 393224 | tf_op jit(solution)/shard_map/ppermute | solution.py:127
  58.7 0.2 collective-permute-done.17
  58.9 0.3 fusion.17
  59.3 0.2 fusion.3
  59.5 0.3 convolution_convert_fusion
  59.8 3.2 %collective-permute-done.22 = bf16[4,16,3072]{2,1,0:T(8,128)(2,1)S(1)} collective-permute-done((bf16[4,16,3072]{2,1,0:T(8,128)(2,1)S(1)}, bf16[4,16,3072]{2,1,0:T(8,128)(2,1)S(1)}, u32[]{:S(2)}, u32[]{:S(2)}) %collective-permute-start.22) | collective-permute-done | bytes 393248 | tf_op jit(solution)/shard_map/ppermute | solution.py:127
  63.0 8.0 %collective-permute-done.23 = bf16[4,16,3072]{2,1,0:T(8,128)(2,1)S(1)} collective-permute-done((bf16[4,16,3072]{2,1,0:T(8,128)(2,1)S(1)}, bf16[4,16,3072]{2,1,0:T(8,128)(2,1)S(1)}, u32[]{:S(2)}, u32[]{:S(2)}) %collective-permute-start.23) | collective-permute-done | bytes 393248 | tf_op jit(solution)/shard_map/ppermute | solution.py:127
  71.1 0.5 collective-permute-start.26
  71.6 0.1 collective-permute-start.27
  71.8 0.5 collective-permute-start.28
  72.3 0.3 fusion.16
  72.7 0.2 fusion.2
  72.9 0.3 convolution_convert_fusion.1
  73.2 1.6 %collective-permute-start.18 = (bf16[128,256]{0,1:T(8,128)(2,1)S(1)}, bf16[128,256]{0,1:T(8,128)(2,1)S(1)}, u32[]{:S(2)}, u32[]{:S(2)}) collective-permute-start(bf16[128,256]{0,1:T(8,128)(2,1)S(1)} %get-tuple-element.38), channel_id=1, source_target_pairs={{0,1},{1,0},{2,3},{3,2},{4,5},{5,4},{6,7},{7,6},{8,9},{9,8},{10,11... | collective-permute-start | bytes 196616 | tf_op jit(solution)/shard_map/ppermute | solution.py:127
  75.0 2.6 %collective-permute-done.18 = bf16[128,256]{0,1:T(8,128)(2,1)S(1)} collective-permute-done((bf16[128,256]{0,1:T(8,128)(2,1)S(1)}, bf16[128,256]{0,1:T(8,128)(2,1)S(1)}, u32[]{:S(2)}, u32[]{:S(2)}) %collective-permute-start.18) | collective-permute-done | bytes 65568 | tf_op jit(solution)/shard_map/ppermute | solution.py:127
  77.6 1.5 %fusion.1 = bf16[1,128,3072]{2,1,0:T(8,128)(2,1)} fusion(bf16[512,3072]{1,0:T(8,128)(2,1)S(1)} %bitcast.34, f32[3072]{0:T(1024)S(1)} %bitcast.41, bf16[128,256]{0,1:T(8,128)(2,1)S(1)} %collective-permute-done.18, bf16[128,256]{0,1:T(8,128)(2,1)S(1)} %get-tuple-element.37), kind=kOutput, calls=%fused_computation.2 | convolution fusion | flops 403701760 | bytes 4075520 | tf_op jit(solution)/shard_map/dot_general | solution.py:208
  (58 shorter events, 0.6 us)
Async XLA Ops:
  0.0 11.4 %copy-start = (bf16[1,128,3072]{2,1,0:T(8,128)(2,1)S(1)}, bf16[1,128,3072]{2,1,0:T(8,128)(2,1)}, u32[]{:S(2)}) copy-start(bf16[1,128,3072]{2,1,0:T(8,128)(2,1)} %param.5) | copy-start | bytes 2359300
  0.0 11.4 %collective-permute-start.1 = (bf16[384,384]{1,0:T(8,128)(2,1)}, bf16[384,384]{1,0:T(8,128)(2,1)S(1)}, u32[]{:S(2)}, u32[]{:S(2)}) collective-permute-start(bf16[384,384]{1,0:T(8,128)(2,1)} %bitcast.28), channel_id=1, source_target_pairs={{0,8},{1,9},{2,10},{3,11},{4,12},{5,13},{6,14},{7,15},{8,0},{9,1},... | collective-permute-start | bytes 884744 | tf_op jit(solution)/shard_map/ppermute | solution.py:127
  3.0 15.0 %collective-permute-start.2 = (bf16[384,384]{1,0:T(8,128)(2,1)}, bf16[384,384]{1,0:T(8,128)(2,1)S(1)}, u32[]{:S(2)}, u32[]{:S(2)}) collective-permute-start(bf16[384,384]{1,0:T(8,128)(2,1)} %bitcast.29), channel_id=1, source_target_pairs={{0,16},{1,17},{2,18},{3,19},{4,20},{5,21},{6,22},{7,23},{8,24},{9,... | collective-permute-start | bytes 884744 | tf_op jit(solution)/shard_map/ppermute | solution.py:127
  4.5 19.9 %collective-permute-start.3 = (bf16[384,384]{1,0:T(8,128)(2,1)}, bf16[384,384]{1,0:T(8,128)(2,1)}, u32[]{:S(2)}, u32[]{:S(2)}) collective-permute-start(bf16[384,384]{1,0:T(8,128)(2,1)} %bitcast.30), channel_id=1, source_target_pairs={{0,24},{1,25},{2,26},{3,27},{4,28},{5,29},{6,30},{7,31},{8,16},{9,... | collective-permute-start | bytes 884744 | tf_op jit(solution)/shard_map/ppermute | solution.py:127
  4.5 21.6 %collective-permute-start.4 = (bf16[384,384]{1,0:T(8,128)(2,1)}, bf16[384,384]{1,0:T(8,128)(2,1)}, u32[]{:S(2)}, u32[]{:S(2)}) collective-permute-start(bf16[384,384]{1,0:T(8,128)(2,1)} %bitcast.31), channel_id=1, source_target_pairs={{0,4},{1,5},{2,6},{3,7},{4,0},{5,1},{6,2},{7,3},{8,12},{9,13},{10,... | collective-permute-start | bytes 884744 | tf_op jit(solution)/shard_map/ppermute | solution.py:127
  4.5 17.4 %collective-permute-start.8 = (bf16[384,384]{1,0:T(8,128)(2,1)}, bf16[384,384]{1,0:T(8,128)(2,1)S(1)}, u32[]{:S(2)}, u32[]{:S(2)}) collective-permute-start(bf16[384,384]{1,0:T(8,128)(2,1)} %bitcast.32), channel_id=1, source_target_pairs={{0,2},{1,3},{2,0},{3,1},{4,6},{5,7},{6,4},{7,5},{8,10},{9,11},{10,... | collective-permute-start | bytes 884744 | tf_op jit(solution)/shard_map/ppermute | solution.py:127
  8.3 37.5 %copy-start.1 = (bf16[1,384,384]{2,1,0:T(8,128)(2,1)S(1)}, bf16[1,384,384]{2,1,0:T(8,128)(2,1)}, u32[]{:S(2)}) copy-start(bf16[1,384,384]{2,1,0:T(8,128)(2,1)} %param.8) | copy-start | bytes 884740
  11.4 29.7 %collective-permute-start = (bf16[128,3072]{1,0:T(8,128)(2,1)S(1)}, bf16[128,3072]{1,0:T(8,128)(2,1)S(1)}, u32[]{:S(2)}, u32[]{:S(2)}) collective-permute-start(bf16[128,3072]{1,0:T(8,128)(2,1)S(1)} %bitcast.26), channel_id=1, source_target_pairs={{0,1},{1,0},{2,3},{3,2},{4,5},{5,4},{6,7},{7,6},{8,9},{9,8},{10,11... | collective-permute-start | bytes 2359304 | tf_op jit(solution)/shard_map/ppermute | solution.py:127
  18.0 10.2 %collective-permute-start.5 = (bf16[384,384]{1,0:T(8,128)(2,1)S(1)}, bf16[384,384]{1,0:T(8,128)(2,1)}, u32[]{:S(2)}, u32[]{:S(2)}) collective-permute-start(bf16[384,384]{1,0:T(8,128)(2,1)S(1)} %collective-permute-done.1.refs_3_), channel_id=1, source_target_pairs={{0,4},{1,5},{2,6},{3,7},{4,0},{5,1},{6,2},{7,3},{8,12},{9,13},{10,... | collective-permute-start | bytes 884744 | tf_op jit(solution)/shard_map/ppermute | solution.py:127
  21.9 7.8 %collective-permute-start.6 = (bf16[384,384]{1,0:T(8,128)(2,1)S(1)}, bf16[384,384]{1,0:T(8,128)(2,1)}, u32[]{:S(2)}, u32[]{:S(2)}) collective-permute-start(bf16[384,384]{1,0:T(8,128)(2,1)S(1)} %collective-permute-done.2.refs_4_), channel_id=1, source_target_pairs={{0,4},{1,5},{2,6},{3,7},{4,0},{5,1},{6,2},{7,3},{8,12},{9,13},{10,... | collective-permute-start | bytes 884744 | tf_op jit(solution)/shard_map/ppermute | solution.py:127
  22.6 0.7 copy-start.2
  24.4 15.9 %collective-permute-start.10 = (bf16[384,384]{1,0:T(8,128)(2,1)S(1)}, bf16[384,384]{1,0:T(8,128)(2,1)}, u32[]{:S(2)}, u32[]{:S(2)}) collective-permute-start(bf16[384,384]{1,0:T(8,128)(2,1)S(1)} %collective-permute-done.8.refs_2_), channel_id=1, source_target_pairs={{0,16},{1,17},{2,18},{3,19},{4,20},{5,21},{6,22},{7,23},{8,24},{9,... | collective-permute-start | bytes 884744 | tf_op jit(solution)/shard_map/ppermute | solution.py:127
  26.1 4.6 %collective-permute-start.7 = (bf16[384,384]{1,0:T(8,128)(2,1)}, bf16[384,384]{1,0:T(8,128)(2,1)}, u32[]{:S(2)}, u32[]{:S(2)}) collective-permute-start(bf16[384,384]{1,0:T(8,128)(2,1)} %collective-permute-done.3.refs_5_), channel_id=1, source_target_pairs={{0,4},{1,5},{2,6},{3,7},{4,0},{5,1},{6,2},{7,3},{8,12},{9,13},{10,... | collective-permute-start | bytes 884744 | tf_op jit(solution)/shard_map/ppermute | solution.py:127
  28.2 20.3 %collective-permute-start.11 = (bf16[384,384]{1,0:T(8,128)(2,1)S(1)}, bf16[384,384]{1,0:T(8,128)(2,1)S(1)}, u32[]{:S(2)}, u32[]{:S(2)}) collective-permute-start(bf16[384,384]{1,0:T(8,128)(2,1)S(1)} %collective-permute-done.8.refs_2_), channel_id=1, source_target_pairs={{0,24},{1,25},{2,26},{3,27},{4,28},{5,29},{6,30},{7,31},{8,16},{9,... | collective-permute-start | bytes 884744 | tf_op jit(solution)/shard_map/ppermute | solution.py:127
  29.6 18.9 %collective-permute-start.9 = (bf16[384,384]{1,0:T(8,128)(2,1)S(1)}, bf16[384,384]{1,0:T(8,128)(2,1)S(1)}, u32[]{:S(2)}, u32[]{:S(2)}) collective-permute-start(bf16[384,384]{1,0:T(8,128)(2,1)S(1)} %collective-permute-done.8.refs_2_), channel_id=1, source_target_pairs={{0,8},{1,9},{2,10},{3,11},{4,12},{5,13},{6,14},{7,15},{8,0},{9,1},... | collective-permute-start | bytes 884744 | tf_op jit(solution)/shard_map/ppermute | solution.py:127
  30.7 18.4 %collective-permute-start.19 = (bf16[16,3072]{1,0:T(8,128)(2,1)}, bf16[16,3072]{1,0:T(8,128)(2,1)S(1)}, u32[]{:S(2)}, u32[]{:S(2)}) collective-permute-start(bf16[16,3072]{1,0:T(8,128)(2,1)} %bitcast.35), channel_id=1, source_target_pairs={{0,2},{1,3},{2,0},{3,1},{4,6},{5,7},{6,4},{7,5},{8,10},{9,11},{10,... | collective-permute-start | bytes 294920 | tf_op jit(solution)/shard_map/ppermute | solution.py:127
  40.3 8.8 %collective-permute-start.20 = (bf16[16,3072]{1,0:T(8,128)(2,1)}, bf16[16,3072]{1,0:T(8,128)(2,1)S(1)}, u32[]{:S(2)}, u32[]{:S(2)}) collective-permute-start(bf16[16,3072]{1,0:T(8,128)(2,1)} %bitcast.36), channel_id=1, source_target_pairs={{0,1},{1,0},{2,3},{3,2},{4,5},{5,4},{6,7},{7,6},{8,9},{9,8},{10,11... | collective-permute-start | bytes 294920 | tf_op jit(solution)/shard_map/ppermute | solution.py:127
  41.1 8.5 %collective-permute-start.21 = (bf16[16,3072]{1,0:T(8,128)(2,1)}, bf16[16,3072]{1,0:T(8,128)(2,1)S(1)}, u32[]{:S(2)}, u32[]{:S(2)}) collective-permute-start(bf16[16,3072]{1,0:T(8,128)(2,1)} %bitcast.37), channel_id=1, source_target_pairs={{0,3},{1,2},{2,1},{3,0},{4,7},{5,6},{6,5},{7,4},{8,11},{9,10},{10,... | collective-permute-start | bytes 294920 | tf_op jit(solution)/shard_map/ppermute | solution.py:127
  43.9 0.7 copy-start.3
  44.6 5.0 %copy-start.4 = (bf16[1,16,3072]{2,1,0:T(8,128)(2,1)S(1)}, bf16[1,16,3072]{2,1,0:T(8,128)(2,1)}, u32[]{:S(2)}) copy-start(bf16[1,16,3072]{2,1,0:T(8,128)(2,1)} %param.9) | copy-start | bytes 294916
  48.5 2.4 %collective-permute-start.12 = (bf16[384,384]{1,0:T(8,128)(2,1)S(1)}, bf16[384,384]{1,0:T(8,128)(2,1)S(1)}, u32[]{:S(2)}, u32[]{:S(2)}) collective-permute-start(bf16[384,384]{1,0:T(8,128)(2,1)S(1)} %collective-permute-done.8.refs_2_), channel_id=1, source_target_pairs={{0,4},{1,5},{2,6},{3,7},{4,0},{5,1},{6,2},{7,3},{8,12},{9,13},{10,... | collective-permute-start | bytes 884744 | tf_op jit(solution)/shard_map/ppermute | solution.py:127
  48.6 3.9 %collective-permute-start.13 = (bf16[384,384]{1,0:T(8,128)(2,1)S(1)}, bf16[384,384]{1,0:T(8,128)(2,1)S(1)}, u32[]{:S(2)}, u32[]{:S(2)}) collective-permute-start(bf16[384,384]{1,0:T(8,128)(2,1)S(1)} %collective-permute-done.9.refs_3_), channel_id=1, source_target_pairs={{0,4},{1,5},{2,6},{3,7},{4,0},{5,1},{6,2},{7,3},{8,12},{9,13},{10,... | collective-permute-start | bytes 884744 | tf_op jit(solution)/shard_map/ppermute | solution.py:127
  49.1 5.0 %collective-permute-start.14 = (bf16[384,384]{1,0:T(8,128)(2,1)}, bf16[384,384]{1,0:T(8,128)(2,1)S(1)}, u32[]{:S(2)}, u32[]{:S(2)}) collective-permute-start(bf16[384,384]{1,0:T(8,128)(2,1)} %collective-permute-done.10.refs_4_), channel_id=1, source_target_pairs={{0,4},{1,5},{2,6},{3,7},{4,0},{5,1},{6,2},{7,3},{8,12},{9,13},{10,... | collective-permute-start | bytes 884744 | tf_op jit(solution)/shard_map/ppermute | solution.py:127
  49.2 5.4 %collective-permute-start.15 = (bf16[384,384]{1,0:T(8,128)(2,1)S(1)}, bf16[384,384]{1,0:T(8,128)(2,1)S(1)}, u32[]{:S(2)}, u32[]{:S(2)}) collective-permute-start(bf16[384,384]{1,0:T(8,128)(2,1)S(1)} %collective-permute-done.11.refs_5_), channel_id=1, source_target_pairs={{0,4},{1,5},{2,6},{3,7},{4,0},{5,1},{6,2},{7,3},{8,12},{9,13},{10,... | collective-permute-start | bytes 884744 | tf_op jit(solution)/shard_map/ppermute | solution.py:127
  49.7 9.3 %collective-permute-start.17 = (bf16[256,256]{1,0:T(8,128)(2,1)S(1)}, bf16[256,256]{1,0:T(8,128)(2,1)S(1)}, u32[]{:S(2)}, u32[]{:S(2)}) collective-permute-start(bf16[256,256]{1,0:T(8,128)(2,1)S(1)} %get-tuple-element.23), channel_id=1, source_target_pairs={{0,2},{1,3},{2,0},{3,1},{4,6},{5,7},{6,4},{7,5},{8,10},{9,11},{10,... | collective-permute-start | bytes 393224 | tf_op jit(solution)/shard_map/ppermute | solution.py:127
  51.0 12.1 %collective-permute-start.22 = (bf16[4,16,3072]{2,1,0:T(8,128)(2,1)S(1)}, bf16[4,16,3072]{2,1,0:T(8,128)(2,1)S(1)}, u32[]{:S(2)}, u32[]{:S(2)}) collective-permute-start(bf16[4,16,3072]{2,1,0:T(8,128)(2,1)S(1)} %pad_maximum_fusion), channel_id=1, source_target_pairs={{0,8},{1,9},{2,10},{3,11},{4,12},{5,13},{6,14},{7,15},{8,0},{9,1},... | collective-permute-start | bytes 1179656 | tf_op jit(solution)/shard_map/ppermute | solution.py:127
  52.5 18.4 %collective-permute-start.23 = (bf16[4,16,3072]{2,1,0:T(8,128)(2,1)S(1)}, bf16[4,16,3072]{2,1,0:T(8,128)(2,1)S(1)}, u32[]{:S(2)}, u32[]{:S(2)}) collective-permute-start(bf16[4,16,3072]{2,1,0:T(8,128)(2,1)S(1)} %pad_maximum_fusion), channel_id=1, source_target_pairs={{0,16},{1,17},{2,18},{3,19},{4,20},{5,21},{6,22},{7,23},{8,24},{9,... | collective-permute-start | bytes 1179656 | tf_op jit(solution)/shard_map/ppermute | solution.py:127
  54.1 16.9 %collective-permute-start.24 = (bf16[4,16,3072]{2,1,0:T(8,128)(2,1)S(1)}, bf16[4,16,3072]{2,1,0:T(8,128)(2,1)S(1)}, u32[]{:S(2)}, u32[]{:S(2)}) collective-permute-start(bf16[4,16,3072]{2,1,0:T(8,128)(2,1)S(1)} %pad_maximum_fusion), channel_id=1, source_target_pairs={{0,24},{1,25},{2,26},{3,27},{4,28},{5,29},{6,30},{7,31},{8,16},{9,... | collective-permute-start | bytes 1179656 | tf_op jit(solution)/shard_map/ppermute | solution.py:127
  56.9 15.4 %collective-permute-start.16 = (bf16[256,256]{1,0:T(8,128)(2,1)S(1)}, bf16[256,256]{1,0:T(8,128)(2,1)S(1)}, u32[]{:S(2)}, u32[]{:S(2)}) collective-permute-start(bf16[256,256]{1,0:T(8,128)(2,1)S(1)} %get-tuple-element.29), channel_id=1, source_target_pairs={{0,2},{1,3},{2,0},{3,1},{4,6},{5,7},{6,4},{7,5},{8,10},{9,11},{10,... | collective-permute-start | bytes 393224 | tf_op jit(solution)/shard_map/ppermute | solution.py:127
  71.0 3.8 %collective-permute-start.25 = (bf16[4,16,3072]{2,1,0:T(8,128)(2,1)S(1)}, bf16[4,16,3072]{2,1,0:T(8,128)(2,1)S(1)}, u32[]{:S(2)}, u32[]{:S(2)}) collective-permute-start(bf16[4,16,3072]{2,1,0:T(8,128)(2,1)S(1)} %pad_maximum_fusion), channel_id=1, source_target_pairs={{0,4},{1,5},{2,6},{3,7},{4,0},{5,1},{6,2},{7,3},{8,12},{9,13},{10,... | collective-permute-start | bytes 1179656 | tf_op jit(solution)/shard_map/ppermute | solution.py:127
  71.1 3.8 %collective-permute-start.26 = (bf16[4,16,3072]{2,1,0:T(8,128)(2,1)S(1)}, bf16[4,16,3072]{2,1,0:T(8,128)(2,1)S(1)}, u32[]{:S(2)}, u32[]{:S(2)}) collective-permute-start(bf16[4,16,3072]{2,1,0:T(8,128)(2,1)S(1)} %collective-permute-done.22), channel_id=1, source_target_pairs={{0,4},{1,5},{2,6},{3,7},{4,0},{5,1},{6,2},{7,3},{8,12},{9,13},{10,... | collective-permute-start | bytes 1179656 | tf_op jit(solution)/shard_map/ppermute | solution.py:127
  71.6 3.3 %collective-permute-start.27 = (bf16[4,16,3072]{2,1,0:T(8,128)(2,1)S(1)}, bf16[4,16,3072]{2,1,0:T(8,128)(2,1)S(1)}, u32[]{:S(2)}, u32[]{:S(2)}) collective-permute-start(bf16[4,16,3072]{2,1,0:T(8,128)(2,1)S(1)} %collective-permute-done.23), channel_id=1, source_target_pairs={{0,4},{1,5},{2,6},{3,7},{4,0},{5,1},{6,2},{7,3},{8,12},{9,13},{10,... | collective-permute-start | bytes 1179656 | tf_op jit(solution)/shard_map/ppermute | solution.py:127
  71.8 3.2 %collective-permute-start.28 = (bf16[4,16,3072]{2,1,0:T(8,128)(2,1)S(1)}, bf16[4,16,3072]{2,1,0:T(8,128)(2,1)S(1)}, u32[]{:S(2)}, u32[]{:S(2)}) collective-permute-start(bf16[4,16,3072]{2,1,0:T(8,128)(2,1)S(1)} %collective-permute-done.24), channel_id=1, source_target_pairs={{0,4},{1,5},{2,6},{3,7},{4,0},{5,1},{6,2},{7,3},{8,12},{9,13},{10,... | collective-permute-start | bytes 1179656 | tf_op jit(solution)/shard_map/ppermute | solution.py:127
  72.6 4.9 %copy-start.5 = (f32[1,3072]{1,0:T(1,128)S(1)}, f32[1,3072]{1,0:T(1,128)}, u32[]{:S(2)}) copy-start(f32[1,3072]{1,0:T(1,128)} %get-tuple-element.39) | copy-start | bytes 36868
  73.2 4.3 %collective-permute-start.18 = (bf16[128,256]{0,1:T(8,128)(2,1)S(1)}, bf16[128,256]{0,1:T(8,128)(2,1)S(1)}, u32[]{:S(2)}, u32[]{:S(2)}) collective-permute-start(bf16[128,256]{0,1:T(8,128)(2,1)S(1)} %get-tuple-element.38), channel_id=1, source_target_pairs={{0,1},{1,0},{2,3},{3,2},{4,5},{5,4},{6,7},{7,6},{8,9},{9,8},{10,11... | collective-permute-start | bytes 196616 | tf_op jit(solution)/shard_map/ppermute | solution.py:127
